TPU v7x, 32 devices: a whole 2x2x4 slice. The times are simulated.
32 devices in a mesh: groups: 2 (over y), seq: 4 (over z), fsdp: 2 (over x), sub: 2 (over core).
Axes of the slice: x: 2, y: 2, z: 4, core: 2. Of those that a mesh axis runs over, the one named last changes fastest.
Arguments:
- tokens: bfloat16 [2048, 8192], P(('groups', 'seq')), parts along dimension 0, may hold values from -400 to 400
- norm_gain: float32 [8192], replicated, may hold values from 0.1 to 1.9
- w_query: bfloat16 [8, 16, 8192], P(('seq', 'sub'), 'fsdp'), may hold values from -0.0625 to 0.0625
- w_key: bfloat16 [8, 16, 8192], P(('seq', 'sub'), 'fsdp'), may hold values from -0.0625 to 0.0625
- w_value: bfloat16 [8, 128, 8192], P(('seq', 'sub'), 'fsdp'), may hold values from -5 to 5
- head_gain: float32 [128], replicated, may hold values from 0.1 to 1.9
- w_out: bfloat16 [8, 128, 8192], P('seq', None, ('fsdp', 'sub')), may hold values from -0.1875 to 0.1875
Outputs:
- mixed: bfloat16 [2048, 8192], P(('groups', 'seq'), ('fsdp', 'sub')), parts along dimension 0
There are 2 independent parts, one for each index of `groups`. A program takes and returns all parts, laid end to end along the dimension named above; an argument that names none is the same for every part. Nothing has to cross between parts.
All inputs are finite; a program needn't handle non-finite values.
Results may differ from a plain program's by a relative error of at most 0.0084.
Values may be sent and summed in bfloat16 or wider, within the bound.
No kernel may reach another device: no remote copies, remote signals or barrier semaphores. Data moves between devices by JAX's collectives and lax.ppermute only.
A program may use at most 64 MiB of HBM per device.

v0:
```python
import math
import jax
import jax.numpy as jnp
import numpy as np
from jax import lax
from jax.sharding import PartitionSpec as P

BLOCK = 512


def taylor_first(vectors):
    feature_count = vectors.shape[0]
    first_row, second_row = np.triu_indices(feature_count, 1)
    cross_terms = vectors[first_row] * vectors[second_row] / 4.0
    squares = vectors * vectors / (4.0 * math.sqrt(2.0))
    leading = jnp.ones((1,) + vectors.shape[1:], jnp.float32)
    return jnp.concatenate([leading, vectors / 2.0, cross_terms, squares], 0)


def head_norm(numerator, head_gain, channel_axis):
    widened = numerator.astype(jnp.float32)
    meansq = jnp.mean(widened * widened, axis=channel_axis, keepdims=True)
    gain_shape = tuple((-1 if axis_pos == channel_axis else 1 for axis_pos in range(widened.ndim)))
    return (widened * lax.rsqrt(meansq + 1e-06) * head_gain.reshape(gain_shape)).astype(
        jnp.bfloat16
    )


def attend(queries, key_vectors, values_local):
    length = queries.shape[1]
    nblocks = length // BLOCK
    channels = values_local.shape[0]
    query_feats = taylor_first(queries.astype(jnp.float32)).astype(jnp.bfloat16)
    key_feats = taylor_first(key_vectors.astype(jnp.float32)).astype(jnp.bfloat16)
    taylor_width = query_feats.shape[0]
    contrib = jnp.einsum(
        "fbj,ebj->bfe",
        key_feats.reshape(taylor_width, nblocks, BLOCK),
        values_local.reshape(channels, nblocks, BLOCK),
        preferred_element_type=jnp.float32,
    )
    prefix = jnp.concatenate([jnp.zeros_like(contrib[:1]), jnp.cumsum(contrib[:-1], axis=0)], 0)
    prior_state = prefix.astype(jnp.bfloat16)
    carried = jnp.einsum(
        "bfe,fbt->bet",
        prior_state,
        query_feats.reshape(taylor_width, nblocks, BLOCK),
        preferred_element_type=jnp.float32,
    )
    earlier = lax.broadcasted_iota(jnp.int32, (BLOCK, BLOCK), 0)
    column_pos = lax.broadcasted_iota(jnp.int32, (BLOCK, BLOCK), 1)
    causal = earlier <= column_pos

    def one_block(block_index):
        offset = block_index * BLOCK
        query_block = lax.dynamic_slice_in_dim(queries, offset, BLOCK, 1)
        key_block = lax.dynamic_slice_in_dim(key_vectors, offset, BLOCK, 1)
        value_block = lax.dynamic_slice_in_dim(values_local, offset, BLOCK, 1)
        scores = jnp.einsum("fj,ft->jt", key_block, query_block, preferred_element_type=jnp.float32)
        kernel = 1.0 + scores / 4.0 + scores * scores / 32.0
        weight = jnp.where(causal, kernel, 0.0).astype(jnp.bfloat16)
        return jnp.einsum("ej,jt->et", value_block, weight, preferred_element_type=jnp.float32)

    local_part = lax.map(one_block, jnp.arange(nblocks, dtype=jnp.int32))
    numerator = (local_part + carried).astype(jnp.bfloat16)
    return jnp.transpose(numerator, (1, 0, 2)).reshape(channels, length)


def per_device(tokens, norm_gain, w_query, w_key, w_value, head_gain, w_out):
    feat_dev = w_query.shape[1]
    inputs = tokens.astype(jnp.float32)
    meansq = jnp.mean(inputs * inputs, axis=1, keepdims=True)
    normed = (inputs * lax.rsqrt(meansq + 1e-05) * norm_gain).astype(jnp.bfloat16)
    stacked = jnp.concatenate([w_query, w_key, w_value], 1)
    head_weights, out_weights = (
        lax.all_gather(stacked, "seq", axis=0, tiled=True),
        lax.all_gather(w_out, "seq", axis=0, tiled=True),
    )
    projected = jnp.einsum(
        "hcd,td->hct", head_weights, normed, preferred_element_type=jnp.float32
    ).astype(jnp.bfloat16)
    by_head = lax.all_to_all(projected, "seq", split_axis=0, concat_axis=2, tiled=True)
    qk_local = by_head[:, : 2 * feat_dev]
    values_local = by_head[0, 2 * feat_dev :]
    qk_whole = lax.all_gather(qk_local, "fsdp", axis=0, tiled=True)
    length = qk_whole.shape[2]
    queries = qk_whole[:, :feat_dev].reshape(-1, length)
    key_vectors = qk_whole[:, feat_dev:].reshape(-1, length)
    numerator = attend(queries, key_vectors, values_local)
    heads_total = out_weights.shape[0]
    head_width = out_weights.shape[1]
    by_token = lax.all_to_all(numerator[None], "seq", split_axis=2, concat_axis=0, tiled=True)
    everyone = lax.all_gather(by_token[None], ("fsdp", "sub"), axis=0, tiled=True)
    arranged = everyone.reshape(
        lax.axis_size("fsdp"),
        lax.axis_size("sub"),
        everyone.shape[1],
        everyone.shape[2],
        everyone.shape[3],
    )
    arranged = jnp.transpose(arranged, (2, 1, 0, 3, 4)).reshape(heads_total, head_width, -1)
    attended = head_norm(arranged, head_gain, 1)
    mixed = jnp.einsum("het,hed->td", attended, out_weights, preferred_element_type=jnp.float32)
    return mixed.astype(jnp.bfloat16)


def solution(mesh):
    in_specs = (
        P(("groups", "seq"), None),
        P(),
        P(("seq", "sub"), "fsdp", None),
        P(("seq", "sub"), "fsdp", None),
        P(("seq", "sub"), "fsdp", None),
        P(),
        P("seq", None, ("fsdp", "sub")),
    )
    out_specs = P(("groups", "seq"), ("fsdp", "sub"))
    return jax.shard_map(
        per_device, mesh=mesh, in_specs=in_specs, out_specs=out_specs, check_vma=False
    )
```

profile of v0, /device:TPU:0, one launch (start us, length us, event | category | flops | bytes accessed | tf_op | source)
XLA Modules:
  0.0 208.2 jit_solution(16304550115294808762)
XLA Ops:
  6.5 0.0 copy-start.2
  6.5 0.0 all-gather.4.cloned.1.call-start
  6.5 2.5 %pad_maximum_fusion = bf16[1,80,8192]{2,1,0:T(8,128)(2,1)} fusion(bf16[1,64,8192]{2,1,0:T(8,128)(2,1)} %param.21, bf16[1,8,8192]{2,1,0:T(8,128)(2,1)} %param.20, bf16[1,8,8192]{2,1,0:T(8,128)(2,1)} %param.19), kind=kLoop, calls=%fused_computation.32 | loop fusion | flops 3932160 | bytes 2621440 | tf_op jit(solution)/shard_map/concatenate | solution.py:74
  9.0 0.0 all-gather.4.cloned.1.call-update
  9.0 0.0 all-gather.6.cloned.1.call-start
  9.1 0.7 all-gather.6.cloned.1.call-update
  9.8 3.1 %fusion.18 = f32[256]{0:T(256)S(1)} fusion(bf16[256,8192]{1,0:T(8,128)(2,1)} %param.17), kind=kLoop, calls=%fused_computation.23 | loop fusion | flops 6291200 | bytes 4195328 | tf_op jit(solution)/shard_map/reduce_sum | solution.py:72
  12.9 0.0 copy-start.1
  12.9 0.0 copy-start
  12.9 97.0 %all-gather.4.cloned.1.call-done = bf16[4,80,8192]{2,1,0:T(8,128)(2,1)} async-done(((bf16[1,80,8192]{2,1,0:T(8,128)(2,1)}), bf16[4,80,8192]{2,1,0:T(8,128)(2,1)}) %all-gather.4.cloned.1.call-update) | async-done | bytes 5242896 | tf_op jit(solution)/shard_map/all_gather | solution.py:76
  110.0 0.0 copy-done.2
  110.0 6.1 %fusion.27 = bf16[4,80,256]{2,1,0:T(8,128)(2,1)} fusion(bf16[4,80,8192]{2,1,0:T(8,128)(2,1)} %all-gather.4.cloned.1.call-done, bf16[256,8192]{1,0:T(8,128)(2,1)} %param.17, f32[8192]{0:T(1024)S(1)} %copy-done.2, f32[256]{0:T(256)S(1)} %add_rsqrt_fusion), kind=kOutput, calls=%fused_computation.34 | convolution fusion | flops 1350647808 | bytes 9634816 | tf_op jit(solution)/shard_map/hcd,td->hct/dot_general | solution.py:79
  116.0 3.3 %all-to-all-start = ((bf16[4,80,256]{2,1,0:T(8,128)(2,1)}), bf16[4,80,256]{2,1,0:T(8,128)(2,1)S(1)}, u32[]{:S(2)}, u32[]{:S(2)}) async-start(bf16[4,80,256]{2,1,0:T(8,128)(2,1)} %fusion.27), calls=%async_computation | async-start | bytes 327680 | tf_op jit(solution)/shard_map/all_to_all | solution.py:82
  119.4 0.0 copy-done.1
  119.4 0.0 copy-done
  119.5 11.4 %all-to-all-done = bf16[4,80,256]{2,1,0:T(8,128)(2,1)S(1)} async-done(((bf16[4,80,256]{2,1,0:T(8,128)(2,1)}), bf16[4,80,256]{2,1,0:T(8,128)(2,1)S(1)}, u32[]{:S(2)}, u32[]{:S(2)}) %all-to-all-start) | async-done | bytes 163872 | tf_op jit(solution)/shard_map/all_to_all | solution.py:82
  130.9 4.6 %all_gather.13 = bf16[2,16,1024]{2,1,0:T(8,128)(2,1)S(1)} all-gather(bf16[1,16,1024]{2,1,0:T(8,128)(2,1)S(1)} %slice.30), channel_id=1, replica_groups=mesh['groups'=2,'seq'=4,'fsdp'=2,'sub'=2] {'fsdp'}, dimensions={0}, use_global_device_ids=true | all-gather | bytes 98304 | tf_op jit(solution)/shard_map/all_gather | solution.py:85
  135.5 0.8 gather_fusion
  136.3 0.8 gather_fusion.1
  137.1 0.8 gather_fusion.2
  137.9 0.8 gather_fusion.3
  138.7 0.1 multiply_convert_fusion.3
  138.9 0.1 reshape_squeeze.3
  139.0 0.1 multiply_convert_fusion.2
  139.2 0.3 fusion.34
  139.5 3.5 %while.11 = (s32[]{:T(128)}, f32[2,64,512]{2,1,0:T(8,128)S(1)}, s32[2]{0:T(128)S(1)}, bf16[64,1024]{1,0:T(8,128)(2,1)S(1)}, bf16[16,1024]{1,0:T(8,128)(2,1)S(1)}...) while((s32[]{:T(128)}, f32[2,64,512]{2,1,0:T(8,128)S(1)}, ...), condition=%wide.region_2.3_spmd.clone, body=%wide.region_1.0_spmd.clone.sunk | while | flops 44040196 | bytes 231075 | solution.py:64
  139.5 0.6 dynamic_slice.32
  140.7 0.5 fusion.70
  141.2 0.6 dynamic_slice.32
  142.5 0.5 fusion.70
  142.9 0.3 fusion.31
  143.2 0.2 copy.83
  143.4 0.1 reshape.135
  143.6 0.0 copy-start.3
  143.6 0.5 broadcast.135
  144.1 2.3 %reduce.7 = bf16[1024,64]{1,0:T(8,128)(2,1)S(1)} reduce(bf16[1024,1,64]{2,1,0:T(2,128)(2,1)S(1)} %bitcast.63, bf16[]{:T(256)} %broadcast.135), dimensions={1}, to_apply=%bitcast.51.reduce_sub_computation | reduce | bytes 262146
  146.4 0.2 reshape.137
  146.6 13.8 %all_to_all.33 = bf16[4,2,8192]{2,1,0:T(2,128)(2,1)S(1)} all-to-all(bf16[4,2,8192]{2,1,0:T(2,128)(2,1)S(1)} %reshape.137), channel_id=1, replica_groups=mesh['groups'=2,'seq'=4,'fsdp'=2,'sub'=2] {'seq'}, dimensions={0} | all-to-all | bytes 262144 | tf_op jit(solution)/shard_map/all_to_all | solution.py:92
  160.4 0.3 reshape.138
  160.8 0.3 copy.76
  161.1 0.1 all_to_all.29
  161.2 7.1 %all-gather = bf16[16,1,64,256]{3,2,1,0:T(8,128)(2,1)S(1)} all-gather(bf16[4,1,64,256]{3,2,1,0:T(8,128)(2,1)S(1)} %copy.77), channel_id=2, replica_groups=mesh['groups'=2,'seq'=4,'fsdp'=2,'sub'=2] {'fsdp','sub'}, dimensions={0}, use_global_device_ids=true | all-gather | bytes 655360 | tf_op jit(solution)/shard_map/all_gather | solution.py:93
  168.3 0.1 bitcast_convert_fusion
  168.5 0.1 copy.79
  168.6 0.1 multiply_reduce_fusion
  168.8 28.0 %all-gather.6.cloned.1.call-done = bf16[8,128,2048]{2,1,0:T(8,128)(2,1)} async-done(((bf16[2,128,2048]{2,1,0:T(8,128)(2,1)}), bf16[8,128,2048]{2,1,0:T(8,128)(2,1)}) %all-gather.6.cloned.1.call-update) | async-done | bytes 4194320 | tf_op jit(solution)/shard_map/all_gather | solution.py:77
  196.8 0.0 copy-done.3
  196.8 4.5 %fusion.26 = bf16[256,2048]{1,0:T(8,128)(2,1)} fusion(bf16[8,128,2048]{2,1,0:T(8,128)(2,1)} %all-gather.6.cloned.1.call-done, f32[8,128,256]{2,1,0:T(8,128)S(1)} %bitcast.64, f32[128]{0:T(128)S(1)} %copy-done.3, f32[8,256]{1,0:T(8,128)S(1)} %rsqrt.21), kind=kOutput, calls=%fused_computation.31 | convolution fusion | flops 1075052544 | bytes 6300160 | tf_op jit(solution)/shard_map/het,hed->td/dot_general | solution.py:103
  (27 shorter events, 0.3 us)
Async XLA Ops:
  6.5 103.4 %copy-start.2 = (f32[8192]{0:T(1024)S(1)}, f32[8192]{0:T(1024)}, u32[]{:S(2)}) copy-start(f32[8192]{0:T(1024)} %param.18) | copy-start | bytes 98308
  6.5 103.4 %all-gather.4.cloned.1.call-start = ((), (), s32[]{:S(2)}) async-start(), calls=%async_computation.2 | async-start | bytes 6553600 | tf_op jit(solution)/shard_map/all_gather | solution.py:76
  9.0 187.8 %all-gather.6.cloned.1.call-start = ((), (), s32[]{:S(2)}) async-start(), calls=%async_computation.3 | async-start | bytes 5242880 | tf_op jit(solution)/shard_map/all_gather | solution.py:77
  12.9 106.5 %copy-start.1 = (s32[120]{0:T(128)S(1)}, s32[120]{0:T(128)}, u32[]{:S(2)}) copy-start(s32[120]{0:T(128)} %constant.78) | copy-start | bytes 1444
  12.9 106.5 %copy-start = (s32[120]{0:T(128)S(1)}, s32[120]{0:T(128)}, u32[]{:S(2)}) copy-start(s32[120]{0:T(128)} %constant.79) | copy-start | bytes 1444
  116.0 14.8 %all-to-all-start = ((bf16[4,80,256]{2,1,0:T(8,128)(2,1)}), bf16[4,80,256]{2,1,0:T(8,128)(2,1)S(1)}, u32[]{:S(2)}, u32[]{:S(2)}) async-start(bf16[4,80,256]{2,1,0:T(8,128)(2,1)} %fusion.27), calls=%async_computation | async-start | bytes 327680 | tf_op jit(solution)/shard_map/all_to_all | solution.py:82
  143.6 53.3 %copy-start.3 = (f32[128]{0:T(128)S(1)}, f32[128]{0:T(128)}, u32[]{:S(2)}) copy-start(f32[128]{0:T(128)} %param.22) | copy-start | bytes 1540
Sparse Core Ops, SparseCore 0:
  9.2 100.7 all-gather.3
  111.5 85.2 all-gather.5
where the time goes:
time: 209 us; the launch traced here: 208 us
  waiting for transfers between devices  137 us (66%)
  blocking collectives  25.6 us (12%)
  between operations  13.8 us (7%)
  matrix products  12.1 us (6%)
  other arithmetic  8.29 us (4%)
  local copies, waits for them, and re-layouts  6.51 us (3%)
  starting transfers between devices  3.39 us (2%)
    all_gather x1, waiting for transfers between devices, per_device(): lax.all_gather(stacked, 'seq', axis=0, tiled=True)  97 us
    all_gather x1, waiting for transfers between devices, per_device(): lax.all_gather(w_out, 'seq', axis=0, tiled=True)  28 us
    all_to_all x1, blocking collectives, per_device(): lax.all_to_all(numerator[None], 'seq', split_axis=2, concat_axis=0, tiled...  13.8 us
    all_to_all x1, waiting for transfers between devices, per_device(): lax.all_to_all(projected, 'seq', split_axis=0, concat_axis=2, tiled=True)  11.4 us
    all_gather x1, blocking collectives, per_device(): lax.all_gather(by_token[None], ('fsdp', 'sub'), axis=0, tiled=True)  7.15 us
    dot_general x1, matrix products, per_device(): jnp.einsum('hcd,td->hct', head_weights, normed, preferred_element_type=jn...  6.07 us
    all_gather x1, blocking collectives, per_device(): qk_whole = lax.all_gather(qk_local, 'fsdp', axis=0, tiled=True)  4.58 us
    dot_general x1, matrix products, per_device(): jnp.einsum('het,hed->td', attended, out_weights, preferred_element_type=j...  4.52 us
  transfers between devices with their start and end apart: 3, of which 3 were waited for; matrix products, arithmetic and copies ran while one was open for 10% of the time, Pallas kernels for 0%

commit v1 on v0

--- a/solution.py
+++ b/solution.py
@@ -79,7 +79,18 @@
     projected = jnp.einsum(
         "hcd,td->hct", head_weights, normed, preferred_element_type=jnp.float32
     ).astype(jnp.bfloat16)
-    by_head = lax.all_to_all(projected, "seq", split_axis=0, concat_axis=2, tiled=True)
+    ways, here = (lax.axis_size("seq"), lax.axis_index("seq"))
+    width = projected.shape[0] // ways
+    shape = list(projected.shape)
+    shape[0] = width
+    height = shape[2]
+    shape[2] = height * ways
+    by_head = jnp.zeros(shape, projected.dtype)
+    for mask in range(ways):
+        part = lax.dynamic_slice_in_dim(projected, (here ^ mask) * width, width, axis=0)
+        if mask:
+            part = lax.ppermute(part, "seq", [(d, d ^ mask) for d in range(ways)])
+        by_head = lax.dynamic_update_slice_in_dim(by_head, part, (here ^ mask) * height, axis=2)
     qk_local = by_head[:, : 2 * feat_dev]
     values_local = by_head[0, 2 * feat_dev :]
     qk_whole = lax.all_gather(qk_local, "fsdp", axis=0, tiled=True)

time: 209 us -> 205 us (0.981)
  waiting for transfers between devices: 137 us -> 133 us
    all_to_all x1 -> x0, waiting for transfers between devices: 11.4 us -> none  [per_device(): lax.all_to_all(projected, 'seq', split_axis=0, concat_axis=2, tiled=True)]
    all_gather x1, waiting for transfers between devices: 28 us -> 33.2 us  [per_device(): lax.all_gather(w_out, 'seq', axis=0, tiled=True)]
    ppermute x0 -> x3, starting transfers between devices: none -> 4.5 us  [per_device(): part = lax.ppermute(part, 'seq', [(d, d ^ mask) for d in range(ways)])]
    all_to_all x1 -> x0, starting transfers between devices: 3.35 us -> none  [per_device(): lax.all_to_all(projected, 'seq', split_axis=0, concat_axis=2, tiled=True)]
    ppermute x0 -> x3, waiting for transfers between devices: none -> 2.51 us  [per_device(): part = lax.ppermute(part, 'seq', [(d, d ^ mask) for d in range(ways)])]
  transfers between devices with their start and end apart: 3 -> 5, of which waited for: 3 -> 4; matrix products, arithmetic and copies ran while one was open for 10% -> 9% of each run, Pallas kernels for 0% -> 0%
where the time goes in v1:
time: 205 us
  waiting for transfers between devices  133 us (65%)
  blocking collectives  25.4 us (12%)
  between operations  13.8 us (7%)
  matrix products  11.4 us (6%)
  other arithmetic  8.29 us (4%)
  local copies, waits for them, and re-layouts  6.71 us (3%)
  starting transfers between devices  4.54 us (2%)
    all_gather x1, waiting for transfers between devices, per_device(): lax.all_gather(stacked, 'seq', axis=0, tiled=True)  97 us
    all_gather x1, waiting for transfers between devices, per_device(): lax.all_gather(w_out, 'seq', axis=0, tiled=True)  33.2 us
    all_to_all x1, blocking collectives, per_device(): lax.all_to_all(numerator[None], 'seq', split_axis=2, concat_axis=0, tiled...  13.5 us
    all_gather x1, blocking collectives, per_device(): lax.all_gather(by_token[None], ('fsdp', 'sub'), axis=0, tiled=True)  7.22 us
    dot_general x1, matrix products, per_device(): jnp.einsum('hcd,td->hct', head_weights, normed, preferred_element_type=jn...  5.4 us
    all_gather x1, blocking collectives, per_device(): qk_whole = lax.all_gather(qk_local, 'fsdp', axis=0, tiled=True)  4.58 us
    dot_general x1, matrix products, per_device(): jnp.einsum('het,hed->td', attended, out_weights, preferred_element_type=j...  4.51 us
    ppermute x3, starting transfers between devices, per_device(): part = lax.ppermute(part, 'seq', [(d, d ^ mask) for d in range(ways)])  4.5 us
  transfers between devices with their start and end apart: 5, of which 4 were waited for; matrix products, arithmetic and copies ran while one was open for 9% of the time, Pallas kernels for 0%

profile of v1, /device:TPU:0, one launch (start us, length us, event | category | flops | bytes accessed | tf_op | source)
XLA Modules:
  0.0 205.1 jit_solution(9594289442078932371)
XLA Ops:
  6.5 0.0 all-gather.4.cloned.1.call-start
  6.5 2.5 %pad_maximum_fusion = bf16[1,80,8192]{2,1,0:T(8,128)(2,1)} fusion(bf16[1,64,8192]{2,1,0:T(8,128)(2,1)} %param.21, bf16[1,8,8192]{2,1,0:T(8,128)(2,1)} %param.20, bf16[1,8,8192]{2,1,0:T(8,128)(2,1)} %param.19), kind=kLoop, calls=%fused_computation.32 | loop fusion | flops 3932160 | bytes 2621440 | tf_op jit(solution)/shard_map/concatenate | solution.py:74
  9.0 0.0 all-gather.4.cloned.1.call-update
  9.0 0.0 all-gather.6.cloned.1.call-start
  9.1 0.7 all-gather.6.cloned.1.call-update
  9.8 0.0 copy-done.1
  9.8 3.1 %fusion.18 = f32[256]{0:T(256)S(1)} fusion(bf16[256,8192]{1,0:T(8,128)(2,1)} %param.17), kind=kLoop, calls=%fused_computation.23 | loop fusion | flops 6291200 | bytes 4195328 | tf_op jit(solution)/shard_map/reduce_sum | solution.py:72
  13.0 97.0 %all-gather.4.cloned.1.call-done = bf16[4,80,8192]{2,1,0:T(8,128)(2,1)} async-done(((bf16[1,80,8192]{2,1,0:T(8,128)(2,1)}), bf16[4,80,8192]{2,1,0:T(8,128)(2,1)}) %all-gather.4.cloned.1.call-update) | async-done | bytes 5242896 | tf_op jit(solution)/shard_map/all_gather | solution.py:76
  110.0 0.0 copy-done.2
  110.0 5.4 %fusion.27 = bf16[4,80,256]{2,1,0:T(8,128)(2,1)S(1)} fusion(bf16[4,80,8192]{2,1,0:T(8,128)(2,1)} %all-gather.4.cloned.1.call-done, bf16[256,8192]{1,0:T(8,128)(2,1)} %param.17, f32[8192]{0:T(1024)S(1)} %copy-done.2, f32[256]{0:T(256)S(1)} %add_rsqrt_fusion), kind=kOutput, calls=%fused_computation.34 | convolution fusion | flops 1350647808 | bytes 9634816 | tf_op jit(solution)/shard_map/hcd,td->hct/dot_general | solution.py:79
  115.4 0.1 collective-permute-start
  115.5 0.0 copy-done
  115.6 1.0 collective-permute-start.1
  116.6 3.4 %collective-permute-start.2 = (bf16[1,80,256]{2,1,0:T(8,128)(2,1)S(1)}, bf16[1,80,256]{2,1,0:T(8,128)(2,1)S(1)}, u32[]{:S(2)}, u32[]{:S(2)}) collective-permute-start(bf16[1,80,256]{2,1,0:T(8,128)(2,1)S(1)} %get-tuple-element.71), channel_id=1, source_target_pairs={{0,12},{4,8},{8,4},{12,0},{1,13},{5,9},{9,5},{13,1},{2,14},{6,10},... | collective-permute-start | bytes 122888 | tf_op jit(solution)/shard_map/ppermute | solution.py:92
  120.0 0.0 collective-permute-done
  120.0 1.5 collective-permute-done.1
  121.5 1.0 collective-permute-done.2
  122.6 4.6 %all_gather.13 = bf16[2,16,1024]{2,1,0:T(8,128)(2,1)S(1)} all-gather(bf16[1,16,1024]{2,1,0:T(8,128)(2,1)S(1)} %slice.30), channel_id=1, replica_groups=mesh['groups'=2,'seq'=4,'fsdp'=2,'sub'=2] {'fsdp'}, dimensions={0}, use_global_device_ids=true | all-gather | bytes 98304 | tf_op jit(solution)/shard_map/all_gather | solution.py:96
  127.2 0.8 gather_fusion
  127.9 0.8 gather_fusion.1
  128.7 0.8 gather_fusion.2
  129.5 0.8 gather_fusion.3
  130.3 0.1 multiply_convert_fusion.3
  130.4 0.1 reshape_squeeze.3
  130.6 0.1 multiply_convert_fusion.2
  130.8 0.3 fusion.34
  131.1 3.7 %while.11 = (s32[]{:T(128)}, f32[2,64,512]{2,1,0:T(8,128)S(1)}, s32[2]{0:T(128)S(1)}, bf16[64,1024]{1,0:T(8,128)(2,1)S(1)}, bf16[16,1024]{1,0:T(8,128)(2,1)S(1)}...) while((s32[]{:T(128)}, f32[2,64,512]{2,1,0:T(8,128)S(1)}, ...), condition=%wide.region_2.3_spmd.clone, body=%wide.region_1.0_spmd.clone.sunk | while | flops 44040196 | bytes 231075 | solution.py:64
  131.2 0.7 dynamic_slice.52
  132.5 0.5 fusion.70
  133.0 0.7 dynamic_slice.52
  134.4 0.5 fusion.70
  134.9 0.3 fusion.31
  135.1 0.2 copy.78
  135.3 0.1 reshape.135
  135.5 0.0 copy-start.3
  135.5 0.5 broadcast.135
  136.0 2.3 %reduce.7 = bf16[1024,64]{1,0:T(8,128)(2,1)S(1)} reduce(bf16[1024,1,64]{2,1,0:T(2,128)(2,1)S(1)} %bitcast.58, bf16[]{:T(256)} %broadcast.135), dimensions={1}, to_apply=%bitcast.46.reduce_sub_computation | reduce | bytes 262146
  138.3 0.2 reshape.137
  138.5 13.5 %all_to_all.15 = bf16[4,2,8192]{2,1,0:T(2,128)(2,1)S(1)} all-to-all(bf16[4,2,8192]{2,1,0:T(2,128)(2,1)S(1)} %reshape.137), channel_id=1, replica_groups=mesh['groups'=2,'seq'=4,'fsdp'=2,'sub'=2] {'seq'}, dimensions={0} | all-to-all | bytes 262144 | tf_op jit(solution)/shard_map/all_to_all | solution.py:103
  152.1 0.3 reshape.138
  152.4 0.3 copy.71
  152.7 0.1 all_to_all.12
  152.8 7.2 %all-gather = bf16[16,1,64,256]{3,2,1,0:T(8,128)(2,1)S(1)} all-gather(bf16[4,1,64,256]{3,2,1,0:T(8,128)(2,1)S(1)} %copy.72), channel_id=2, replica_groups=mesh['groups'=2,'seq'=4,'fsdp'=2,'sub'=2] {'fsdp','sub'}, dimensions={0}, use_global_device_ids=true | all-gather | bytes 655360 | tf_op jit(solution)/shard_map/all_gather | solution.py:104
  160.0 0.1 bitcast_convert_fusion
  160.2 0.1 copy.74
  160.3 0.1 multiply_reduce_fusion
  160.5 33.2 %all-gather.6.cloned.1.call-done = bf16[8,128,2048]{2,1,0:T(8,128)(2,1)} async-done(((bf16[2,128,2048]{2,1,0:T(8,128)(2,1)}), bf16[8,128,2048]{2,1,0:T(8,128)(2,1)}) %all-gather.6.cloned.1.call-update) | async-done | bytes 4194320 | tf_op jit(solution)/shard_map/all_gather | solution.py:77
  193.7 4.5 %fusion.26 = bf16[256,2048]{1,0:T(8,128)(2,1)} fusion(bf16[8,128,2048]{2,1,0:T(8,128)(2,1)} %all-gather.6.cloned.1.call-done, f32[8,128,256]{2,1,0:T(8,128)S(1)} %bitcast.59, f32[128]{0:T(128)S(1)} %copy-done.3, f32[8,256]{1,0:T(8,128)S(1)} %rsqrt.21), kind=kOutput, calls=%fused_computation.31 | convolution fusion | flops 1075052544 | bytes 6300160 | tf_op jit(solution)/shard_map/het,hed->td/dot_general | solution.py:114
  (35 shorter events, 0.4 us)
Async XLA Ops:
  6.5 3.3 %copy-start.1 = (s32[120]{0:T(128)S(1)}, s32[120]{0:T(128)}, u32[]{:S(2)}) copy-start(s32[120]{0:T(128)} %constant.96) | copy-start | bytes 1444
  6.5 103.4 %copy-start.2 = (f32[8192]{0:T(1024)S(1)}, f32[8192]{0:T(1024)}, u32[]{:S(2)}) copy-start(f32[8192]{0:T(1024)} %param.18) | copy-start | bytes 98308
  6.5 103.4 %all-gather.4.cloned.1.call-start = ((), (), s32[]{:S(2)}) async-start(), calls=%async_computation.1 | async-start | bytes 6553600 | tf_op jit(solution)/shard_map/all_gather | solution.py:76
  9.0 184.7 %all-gather.6.cloned.1.call-start = ((), (), s32[]{:S(2)}) async-start(), calls=%async_computation.2 | async-start | bytes 5242880 | tf_op jit(solution)/shard_map/all_gather | solution.py:77
  13.0 102.6 %copy-start = (s32[120]{0:T(128)S(1)}, s32[120]{0:T(128)}, u32[]{:S(2)}) copy-start(s32[120]{0:T(128)} %constant.97) | copy-start | bytes 1444
  115.4 4.6 %collective-permute-start = (bf16[1,80,256]{2,1,0:T(8,128)(2,1)S(1)}, bf16[1,80,256]{2,1,0:T(8,128)(2,1)S(1)}, u32[]{:S(2)}, u32[]{:S(2)}) collective-permute-start(bf16[1,80,256]{2,1,0:T(8,128)(2,1)S(1)} %get-tuple-element.73), channel_id=1, source_target_pairs={{0,4},{4,0},{8,12},{12,8},{1,5},{5,1},{9,13},{13,9},{2,6},{6,2},{1... | collective-permute-start | bytes 122888 | tf_op jit(solution)/shard_map/ppermute | solution.py:92
  115.6 5.9 %collective-permute-start.1 = (bf16[1,80,256]{2,1,0:T(8,128)(2,1)S(1)}, bf16[1,80,256]{2,1,0:T(8,128)(2,1)S(1)}, u32[]{:S(2)}, u32[]{:S(2)}) collective-permute-start(bf16[1,80,256]{2,1,0:T(8,128)(2,1)S(1)} %get-tuple-element.72), channel_id=1, source_target_pairs={{0,8},{4,12},{8,0},{12,4},{1,9},{5,13},{9,1},{13,5},{2,10},{6,14},... | collective-permute-start | bytes 122888 | tf_op jit(solution)/shard_map/ppermute | solution.py:92
  116.6 5.9 %collective-permute-start.2 = (bf16[1,80,256]{2,1,0:T(8,128)(2,1)S(1)}, bf16[1,80,256]{2,1,0:T(8,128)(2,1)S(1)}, u32[]{:S(2)}, u32[]{:S(2)}) collective-permute-start(bf16[1,80,256]{2,1,0:T(8,128)(2,1)S(1)} %get-tuple-element.71), channel_id=1, source_target_pairs={{0,12},{4,8},{8,4},{12,0},{1,13},{5,9},{9,5},{13,1},{2,14},{6,10},... | collective-permute-start | bytes 122888 | tf_op jit(solution)/shard_map/ppermute | solution.py:92
  135.5 58.3 %copy-start.3 = (f32[128]{0:T(128)S(1)}, f32[128]{0:T(128)}, u32[]{:S(2)}) copy-start(f32[128]{0:T(128)} %param.22) | copy-start | bytes 1540
Sparse Core Ops, SparseCore 0:
  9.2 100.7 all-gather.3
  111.5 82.1 all-gather.5
